TPU v7x, 32 devices: a whole 2x2x4 slice. The times are simulated.
32 devices in a mesh: dp: 8 (over z, y), expert: 2 (over core), tensor: 2 (over x).
Axes of the slice: x: 2, y: 2, z: 4, core: 2. Of those that a mesh axis runs over, the one named last changes fastest.
Arguments:
- dense_act: bfloat16 [2, 32, 512, 3584], P(None, 'dp', 'expert', 'tensor'), may hold values from -6 to 6
- dense_cot: bfloat16 [2, 32, 512, 3584], P(None, 'dp', ('expert', 'tensor')), may hold values from -6 to 6
- dense_proj_in: bfloat16 [2, 3584, 128], P(None, 'tensor'), may hold values from -0.09375 to 0.09375
- dense_proj_out: bfloat16 [2, 3584, 128], replicated, may hold values from -0.09375 to 0.09375
- expert_act: bfloat16 [32, 8, 64, 2560], P('dp', 'expert', None, 'tensor'), may hold values from -6 to 6
- expert_cot: bfloat16 [32, 8, 64, 3584], P('dp', 'expert', 'tensor'), may hold values from -6 to 6
- expert_proj_in: bfloat16 [2560, 128], P('tensor'), may hold values from -0.125 to 0.125
- expert_proj_out: bfloat16 [3584, 128], replicated, may hold values from -0.09375 to 0.09375
- dense_valid: float32 [2, 128, 128], replicated, may hold values from -0.0012207031 to 0.0012207031
- expert_valid: float32 [8, 128, 128], P('expert'), may hold values from -0.0012207031 to 0.0012207031
- domain_ids: int32 [32], P('dp'), may hold values from 0 to 63
- prior_mix: float32 [64], replicated, may hold values from 0.002 to 0.05
Outputs:
- log_mixture_weights: float32 [64], P('dp')
All inputs are finite; a program needn't handle non-finite values.
Results may differ from a plain program's by a relative error of at most 0.0003.
Values sent between devices are 32-bit elements; how exact they have to be, the bound alone decides.
A program may use at most 128 MiB of HBM per device.

v0:
```python
import functools

import jax
import jax.numpy as jnp
from jax import lax
from jax.experimental import pallas as pl
from jax.experimental.pallas import tpu as pltpu
from jax.sharding import PartitionSpec as P

MESH = pl.DeviceIdType.MESH
HIGHEST = lax.Precision.HIGHEST


def kernel(
    sizes,
    act, cot, pin, pout, eact, ecot, epin, epout, dval, evals, ids, prior,
    out,
    va, vc, vpin, vpout, vea, vec, vepin, vepout, vdv, vev, vids, vprior,
    dsend, drecv, esend, erecv, dg, eg, acc, rows,
    a_sem, c_sem, ea_sem, ec_sem, w_sem,
    ds_sem, dr_sem, es_sem, er_sem, row_send, row_recv,
):
    nd, ne, nt = sizes
    n = nd * ne * nt
    dp, ex, tx = lax.axis_index("dp"), lax.axis_index("expert"), lax.axis_index("tensor")
    me = (dp * ne + ex) * nt + tx
    layers, micro, q, rank = cot.shape[0], cot.shape[1], cot.shape[2], pin.shape[2]
    experts, qc = ecot.shape[1], ecot.shape[2]
    hidden = eact.shape[3]
    dim = ecot.shape[3]

    def split(k):
        return lax.div(k, micro), lax.rem(k, micro)

    def load_a(o, l, m):
        first = pl.multiple_of(lax.rem(tx + o, nt) * q, q)
        return pltpu.make_async_copy(act.at[l, m, pl.ds(first, q), :], va.at[o, l, m], a_sem.at[o, l, m])

    def load_ea(o, m):
        first = pl.multiple_of(lax.rem(tx + o, nt) * qc, qc)
        return pltpu.make_async_copy(eact.at[m, :, pl.ds(first, qc), :], vea.at[o, m], ea_sem.at[o, m])

    def load_c(l, m):
        return pltpu.make_async_copy(cot.at[l, m], vc.at[l, m], c_sem.at[l, m])

    def load_ec(m):
        return pltpu.make_async_copy(ecot.at[m], vec.at[m], ec_sem.at[m])

    weights = [
        pltpu.make_async_copy(src, dst, w_sem.at[i])
        for i, (src, dst) in enumerate(
            [(epin, vepin), (pin, vpin), (pout, vpout), (dval, vdv), (epout, vepout), (evals, vev), (ids, vids), (prior, vprior)]
        )
    ]
    w_epin, w_pin, w_pout, w_dval, w_epout, w_eval, w_ids, w_prior = weights

    def send_d(o, l, m):
        return pltpu.make_async_remote_copy(
            src_ref=dsend.at[o - 1, l, m], dst_ref=drecv.at[o - 1, l, m],
            send_sem=ds_sem.at[o - 1, l, m], recv_sem=dr_sem.at[o - 1, l, m],
            device_id={"dp": dp, "expert": ex, "tensor": lax.rem(tx + o, nt)}, device_id_type=MESH,
        )

    def send_e(o, m):
        return pltpu.make_async_remote_copy(
            src_ref=esend.at[o - 1, m], dst_ref=erecv.at[o - 1, m],
            send_sem=es_sem.at[o - 1, m], recv_sem=er_sem.at[o - 1, m],
            device_id={"dp": dp, "expert": ex, "tensor": lax.rem(tx + o, nt)}, device_id_type=MESH,
        )

    def peer(i):
        t = lax.rem(me + i, n)
        return {"dp": lax.div(t, ne * nt), "expert": lax.rem(lax.div(t, nt), ne), "tensor": lax.rem(t, nt)}

    barrier = pltpu.get_barrier_semaphore()

    @pl.loop(1, n)
    def _(i):
        pl.semaphore_signal(barrier, inc=1, device_id=peer(i), device_id_type=MESH)

    w_epin.start()
    for o in range(1, nt):
        load_ea(o, 0).start()
    for m in range(1, micro):
        for o in range(1, nt):
            load_ea(o, m).start()
    w_pin.start()

    acc[...] = jnp.zeros_like(acc)
    w_epin.wait()

    def expert_out(m):
        for o in range(1, nt):
            load_ea(o, m).wait()
            esend[o - 1, m] = jnp.dot(
                vea[o, m].reshape(experts * qc, hidden), vepin[...], preferred_element_type=jnp.float32
            )
        for l in range(layers):
            for o in range(1, nt):
                load_a(o, l, m).start()

    expert_out(0)
    pl.semaphore_wait(barrier, n - 1)
    for o in range(1, nt):
        send_e(o, 0).start()

    @pl.loop(1, micro)
    def _(m):
        expert_out(m)
        for o in range(1, nt):
            send_e(o, m).start()

    w_pout.start()
    w_dval.start()
    w_pin.wait()

    @pl.loop(0, layers * micro)
    def _(k):
        l, m = split(k)
        for o in range(1, nt):
            load_a(o, l, m).wait()
            dsend[o - 1, l, m] = jnp.dot(va[o, l, m], vpin[l], preferred_element_type=jnp.float32)
        load_a(0, l, m).start()
        load_c(l, m).start()
        for o in range(1, nt):
            send_d(o, l, m).start()

    w_epout.start()
    w_eval.start()
    for m in range(micro):
        load_ea(0, m).start()
        load_ec(m).start()
    w_ids.start()
    w_prior.start()
    w_pout.wait()
    w_dval.wait()

    def fold(m, value):
        acc[m] += jnp.sum(value.reshape(-1, 8, rank), axis=0)

    @pl.loop(0, layers * micro)
    def _(k):
        l, m = split(k)
        load_a(0, l, m).wait()
        load_c(l, m).wait()
        u = jnp.dot(va[0, l, m], vpin[l], preferred_element_type=jnp.float32)
        w = jnp.dot(vc[l, m], vpout[l], preferred_element_type=jnp.float32)
        g = lax.dot_general(
            w, vdv[l], (((1,), (1,)), ((), ())), precision=HIGHEST, preferred_element_type=jnp.float32
        )
        dg[l, m] = g
        fold(m, u * g)

    w_epout.wait()
    w_eval.wait()

    @pl.loop(0, micro)
    def _(m):
        load_ea(0, m).wait()
        load_ec(m).wait()
        u = jnp.dot(vea[0, m].reshape(experts * qc, hidden), vepin[...], preferred_element_type=jnp.float32)
        w = jnp.dot(vec[m].reshape(experts * qc, dim), vepout[...], preferred_element_type=jnp.float32)
        g = jnp.concatenate(
            [
                lax.dot_general(
                    w[e * qc : (e + 1) * qc], vev[e], (((1,), (1,)), ((), ())),
                    precision=HIGHEST, preferred_element_type=jnp.float32,
                )
                for e in range(experts)
            ],
            axis=0,
        )
        eg[m] = g
        fold(m, u * g)

    @pl.loop(0, micro)
    def _(m):
        for o in range(1, nt):
            send_e(o, m).wait()
            fold(m, erecv[o - 1, m] * eg[m])

    w_ids.wait()
    w_prior.wait()

    @pl.loop(0, layers * micro)
    def _(k):
        l, m = split(k)
        for o in range(1, nt):
            send_d(o, l, m).wait()
            fold(m, drecv[o - 1, l, m] * dg[l, m])

    lanes = rows.shape[2]
    lane = lax.broadcasted_iota(jnp.int32, (1, lanes), 1)
    part = jnp.zeros((1, lanes), jnp.float32)
    for m in range(micro):
        score = jnp.sum(jnp.sum(acc[m], axis=0, keepdims=True), axis=1, keepdims=True)
        part = part + jnp.where(lane == vids[m], score, 0.0)
    rows[me] = part

    def send_row(i):
        return pltpu.make_async_remote_copy(
            src_ref=rows.at[me], dst_ref=rows.at[me], send_sem=row_send, recv_sem=row_recv,
            device_id=peer(i), device_id_type=MESH,
        )

    @pl.loop(1, n)
    def _(i):
        send_row(i).start()

    others = rows.at[pl.ds(0, n - 1)]
    pltpu.make_async_copy(others, others, row_recv).wait()
    domains = prior.shape[1]
    total = jnp.sum(rows[...], axis=0)[:, :domains]
    spread = jnp.sqrt(jnp.sum(total * total, axis=1, keepdims=True) * (1.0 / domains) + 1e-06)
    z = total / spread
    mix = vprior[...]
    mass = jnp.sum(mix * jnp.exp(0.5 * z), axis=1, keepdims=True)
    out[...] = jnp.log(mix) + 0.5 * z - jnp.log(mass)
    pltpu.make_async_copy(others, others, row_send).wait()


def per_device(sizes, *args):
    (act, cot, pin, pout, eact, ecot, epin, epout, dval, evals, ids, prior) = args
    nd, ne, nt = sizes
    n = nd * ne * nt
    layers, micro, q, dim = cot.shape
    rank, feat = pin.shape[2], pin.shape[1]
    experts, qc, hidden = ecot.shape[1], ecot.shape[2], eact.shape[3]
    domains = prior.shape[0]
    lanes = -(-domains // 128) * 128
    bf, f32 = jnp.bfloat16, jnp.float32
    V, dma = pltpu.VMEM, pltpu.SemaphoreType.DMA
    logs = pl.pallas_call(
        functools.partial(kernel, sizes),
        out_shape=jax.ShapeDtypeStruct((1, domains), f32),
        in_specs=[pl.BlockSpec(memory_space=pl.ANY)] * 12,
        out_specs=pl.BlockSpec(memory_space=pltpu.VMEM),
        scratch_shapes=[
            V((nt, layers, micro, q, feat), bf),
            V((layers, micro, q, dim), bf),
            V(pin.shape, bf),
            V(pout.shape, bf),
            V((nt, micro, experts, qc, hidden), bf),
            V((micro, experts, qc, dim), bf),
            V(epin.shape, bf),
            V(epout.shape, bf),
            V(dval.shape, f32),
            V(evals.shape, f32),
            pltpu.SMEM(ids.shape, jnp.int32),
            V((1, domains), f32),
            V((nt - 1, layers, micro, q, rank), f32),
            V((nt - 1, layers, micro, q, rank), f32),
            V((nt - 1, micro, experts * qc, rank), f32),
            V((nt - 1, micro, experts * qc, rank), f32),
            V((layers, micro, q, rank), f32),
            V((micro, experts * qc, rank), f32),
            V((micro, 8, rank), f32),
            V((n, 1, lanes), f32),
            dma((nt, layers, micro)),
            dma((layers, micro)),
            dma((nt, micro)),
            dma((micro,)),
            dma((8,)),
            dma((nt - 1, layers, micro)),
            dma((nt - 1, layers, micro)),
            dma((nt - 1, micro)),
            dma((nt - 1, micro)),
            dma,
            dma,
        ],
        compiler_params=pltpu.CompilerParams(
            collective_id=0, has_side_effects=True, vmem_limit_bytes=60 * 1024 * 1024
        ),
        name="align",
    )(act, cot, pin, pout, eact, ecot, epin, epout, dval, evals, ids, prior.reshape(1, domains))
    share = domains // nd
    return lax.dynamic_slice_in_dim(logs[0], lax.axis_index("dp") * share, share, 0)


def solution(mesh):
    sizes = (mesh.shape["dp"], mesh.shape["expert"], mesh.shape["tensor"])
    placed = (
        P(None, "dp", "expert", "tensor"),
        P(None, "dp", ("expert", "tensor"), None),
        P(None, "tensor", None),
        P(),
        P("dp", "expert", None, "tensor"),
        P("dp", "expert", "tensor", None),
        P("tensor", None),
        P(),
        P(),
        P("expert", None, None),
        P("dp"),
        P(),
    )
    return jax.shard_map(
        functools.partial(per_device, sizes), mesh=mesh, in_specs=placed, out_specs=P("dp"), check_vma=False
    )
```

profile of v0, /device:TPU:0, one launch (start us, length us, event | category | flops | bytes accessed | tf_op | source)
XLA Modules:
  0.0 31.8 jit_solution(17670039286888215344)
XLA Ops:
  0.0 30.5 %align.1 = f32[1,64]{1,0:T(1,128)} custom-call(bf16[2,4,256,1792]{3,2,1,0:T(8,128)(2,1)} %act.1, bf16[2,4,128,3584]{3,2,1,0:T(8,128)(2,1)} %cot.1, bf16[2,1792,128]{2,1,0:T(8,128)(2,1)} %pin.1, bf16[2,3584,128]{2,1,0:T(8,128)(2,1)} %pout.1, bf16[4,4,64,1280]{3,2,1,0:T(8,128)(2,1)} %eact.1, bf16[4,4,32,3584]{3,2,1,0:T(8,128)(2,1)} %ecot.1, ...), custom_call_target="tpu_custom_call" | custom-call | tf_op jit(solution)/shard_map/align/pallas_call | solution.py:233
  30.5 1.3 %dynamic-slice_bitcast_fusion = f32[8]{0:T(128)} fusion(f32[1,64]{1,0:T(1,128)} %align.1, s32[]{:T(128)S(6)} %select_n.3), kind=kLoop, calls=%fused_computation | loop fusion | bytes 68 | tf_op jit(solution)/shard_map/dynamic_slice | solution.py:277
where the time goes:
time: 31.9 us; the launch traced here: 31.8 us
  Pallas kernels  30.5 us (96%)
  local copies, waits for them, and re-layouts  1.27 us (4%)
    pallas_call x1, Pallas kernels, per_device(): pl.pallas_call(functools.partial(kernel, sizes), out_shape=jax.ShapeDtype...  30.5 us
    dynamic_slice x1, local copies, waits for them, and re-layouts, per_device(): lax.dynamic_slice_in_dim(logs[0], lax.axis_index('dp') * share, share, 0)  1.27 us

commit v1 on v0

--- a/solution.py
+++ b/solution.py
@@ -232,8 +232,8 @@
     V, dma = pltpu.VMEM, pltpu.SemaphoreType.DMA
     logs = pl.pallas_call(
         functools.partial(kernel, sizes),
-        out_shape=jax.ShapeDtypeStruct((1, domains), f32),
-        in_specs=[pl.BlockSpec(memory_space=pl.ANY)] * 12,
+        out_shape=pltpu.VMEM((1, domains), f32),
+        in_specs=[pl.BlockSpec(memory_space=pltpu.HBM)] * 12,
         out_specs=pl.BlockSpec(memory_space=pltpu.VMEM),
         scratch_shapes=[
             V((nt, layers, micro, q, feat), bf),

time: 31.9 us -> 30.7 us (0.962)
  local copies, waits for them, and re-layouts: 1.27 us -> 0.59 us
  Pallas kernels: 30.5 us -> 29.9 us
    dynamic_slice x1, local copies, waits for them, and re-layouts: 1.27 us -> 0.59 us  [per_device(): lax.dynamic_slice_in_dim(logs[0], lax.axis_index('dp') * share, share, 0)]
    pallas_call x1, Pallas kernels: 30.5 us -> 29.9 us  [per_device(): pl.pallas_call(functools.partial(kernel, sizes), out_shape=pltpu.VMEM((1,...]
where the time goes in v1:
time: 30.7 us; the launch traced here: 30.5 us
  Pallas kernels  29.9 us (97%)
  local copies, waits for them, and re-layouts  0.59 us (2%)
    pallas_call x1, Pallas kernels, per_device(): pl.pallas_call(functools.partial(kernel, sizes), out_shape=pltpu.VMEM((1,...  29.9 us

profile of v1, /device:TPU:0, one launch (start us, length us, event | category | flops | bytes accessed | tf_op | source)
XLA Modules:
  0.0 30.5 jit_solution(5533164575151604979)
XLA Ops:
  0.0 29.9 %align.1 = f32[1,64]{1,0:T(1,128)S(1)} custom-call(bf16[2,4,256,1792]{3,2,1,0:T(8,128)(2,1)} %act.1, bf16[2,4,128,3584]{3,2,1,0:T(8,128)(2,1)} %cot.1, bf16[2,1792,128]{2,1,0:T(8,128)(2,1)} %pin.1, bf16[2,3584,128]{2,1,0:T(8,128)(2,1)} %pout.1, bf16[4,4,64,1280]{3,2,1,0:T(8,128)(2,1)} %eact.1, bf16[4,4,32,3584]{3,2,1,0:T(8,128)(2,1)} %ecot.1, ...), custom_call_target="tpu_custom_call" | custom-call | tf_op jit(solution)/shard_map/align/pallas_call | solution.py:233
  29.9 0.6 %dynamic-slice_bitcast_fusion = f32[8]{0:T(128)} fusion(f32[1,64]{1,0:T(1,128)S(1)} %align.1, s32[]{:T(128)S(6)} %select_n.3), kind=kLoop, calls=%fused_computation | loop fusion | bytes 68 | tf_op jit(solution)/shard_map/dynamic_slice | solution.py:277

commit v2 on v1

v2 whole, which is shorter than its diff:
```python
import functools

import jax
import jax.numpy as jnp
from jax import lax
from jax.experimental import pallas as pl
from jax.experimental.pallas import tpu as pltpu
from jax.sharding import PartitionSpec as P

MESH, LOGICAL = pl.DeviceIdType.MESH, pl.DeviceIdType.LOGICAL
HIGHEST = lax.Precision.HIGHEST
PIECES = 2
LENT = 3
ALONE = 4


def line_of(nd):
    stride = 2 if nd % 2 == 0 else 1
    return stride, nd // stride


def kernel(
    sizes,
    act, cot, pin, pout, eact, ecot, epin, epout, dval, evals, ids, prior,
    out,
    va, vc, vpin, vpout, vea, vec, vepin, vepout, vdv, vev, vids, vprior,
    dsend, drecv, esend, erecv, dg, eg, lu, lg, lmask, mask, acc, rows,
    a_sem, c_sem, ea_sem, w_sem, s_sem, e_sem, d_sem, lu_sem, lg_sem, lg_send, row_send, row_recv,
    line_sem, row_sem, tensor_sem,
):
    nd, ne, nt = sizes
    n = nd * ne * nt
    stride, places = line_of(nd)
    dp, ex, tx = lax.axis_index("dp"), lax.axis_index("expert"), lax.axis_index("tensor")
    me = (dp * ne + ex) * nt + tx
    place, row = lax.div(dp, stride), lax.rem(dp, stride)
    layers, micro, q, rank = cot.shape[0], cot.shape[1], cot.shape[2], pin.shape[2]
    experts, qc = ecot.shape[1], ecot.shape[2]
    hidden = eact.shape[3]
    dim = ecot.shape[3]
    h = q // PIECES
    blocks = layers * micro
    units = blocks * PIECES
    mate = (places - 1 - place) * stride + row

    def lends(at):
        return jnp.where(2 * at >= places, jnp.clip(2 * (at + row - (places + stride) // 2 + 1) - 1, 0, LENT), 0)

    lent, taken = lends(place), lends(places - 1 - place)

    def device(d=None, e=None, t=None):
        return {
            "dp": dp if d is None else d,
            "expert": ex if e is None else e,
            "tensor": tx if t is None else t,
        }

    def load_a(o, l):
        first = pl.multiple_of(lax.rem(tx + o, nt) * q, q)
        return pltpu.make_async_copy(act.at[l, :, pl.ds(first, q), :], va.at[o, l], a_sem.at[l])

    def load_ea(o, first_m, count, i):
        first = pl.multiple_of(lax.rem(tx + o, nt) * qc, qc)
        some = pl.ds(first_m, count)
        return pltpu.make_async_copy(eact.at[some, :, pl.ds(first, qc), :], vea.at[o, some], ea_sem.at[i])

    def load_c(l):
        return pltpu.make_async_copy(cot.at[l], vc.at[l], c_sem.at[l])

    load_ec = pltpu.make_async_copy(ecot, vec, ea_sem.at[1])

    def load_w(src, dst, i):
        return pltpu.make_async_copy(src, dst, w_sem.at[i])

    w_epin, w_pout, w_epout = load_w(epin, vepin, 0), load_w(pout, vpout, 0), load_w(epout, vepout, 0)
    w_pin, w_dval, w_eval = load_w(pin, vpin, 1), load_w(dval, vdv, 1), load_w(evals, vev, 1)
    w_ids, w_prior = load_w(ids, vids, 2), load_w(prior, vprior, 2)

    def rows_of(j, count=1):
        return pl.ds(pl.multiple_of(j * h, h), count * h)

    def opposite(o):
        return lax.rem(tx + o, nt)

    def send_d(o, j):
        i = jnp.minimum(j, LENT) + jnp.maximum(j - (units - ALONE - 1), 0)
        return pltpu.make_async_remote_copy(
            src_ref=dsend.at[o - 1, rows_of(j)], dst_ref=drecv.at[o - 1, rows_of(j)],
            send_sem=s_sem.at[0], recv_sem=d_sem.at[o - 1, i],
            device_id=device(t=opposite(o)), device_id_type=MESH,
        )

    def lend_u(o, j):
        return pltpu.make_async_remote_copy(
            src_ref=dsend.at[o - 1, rows_of(j)], dst_ref=lu.at[o - 1, rows_of(j)],
            send_sem=s_sem.at[0], recv_sem=lu_sem.at[o - 1, j],
            device_id=device(d=mate, t=opposite(o)), device_id_type=MESH,
        )

    def lend_g(j):
        return pltpu.make_async_remote_copy(
            src_ref=dg.at[rows_of(j)], dst_ref=lg.at[rows_of(j)],
            send_sem=lg_send.at[j], recv_sem=lg_sem.at[j],
            device_id=device(d=mate), device_id_type=MESH,
        )

    def lend_mask():
        return pltpu.make_async_remote_copy(
            src_ref=mask, dst_ref=lmask,
            send_sem=lg_send.at[LENT], recv_sem=lg_sem.at[LENT],
            device_id=device(d=mate), device_id_type=MESH,
        )

    def send_e(o, m, e0, count):
        part = pl.ds(e0 * qc, count * qc)
        return pltpu.make_async_remote_copy(
            src_ref=esend.at[o - 1, m, part], dst_ref=erecv.at[o - 1, m, part],
            send_sem=s_sem.at[1], recv_sem=e_sem,
            device_id=device(t=opposite(o)), device_id_type=MESH,
        )

    def landed(ref, sem):
        pltpu.make_async_copy(ref, ref, sem).wait()

    def signal(sem, who):
        pl.semaphore_signal(sem, inc=1, device_id=who, device_id_type=MESH)

    def tell_tensor(sem):
        for o in range(1, nt):
            signal(sem, device(t=opposite(o)))

    def tell_row(sem):
        for j in range(1, stride):
            signal(sem, device(d=place * stride + lax.rem(row + j, stride)))

    def tell_line(sem):
        @pl.when(place > 0)
        def _():
            signal(sem, device(d=dp - stride))

        @pl.when(place < places - 1)
        def _():
            signal(sem, device(d=dp + stride))

    on_line = (place > 0).astype(jnp.int32) + (place < places - 1).astype(jnp.int32)
    line_rounds = places - 1

    def hear_line(r):
        if r < line_rounds:
            pl.semaphore_wait(line_sem.at[r], on_line)

    def next_line(r):
        if r < line_rounds:
            tell_line(line_sem.at[r])

    w_epin.start()
    for o in range(1, nt):
        load_ea(o, 0, 1, 0).start()
    barrier = pltpu.get_barrier_semaphore()
    tell_tensor(barrier)
    for j in range(1, ne):
        signal(barrier, device(e=lax.rem(ex + j, ne)))
    tell_row(barrier)
    tell_line(barrier)
    for o in range(1, nt):
        load_ea(o, 1, micro - 1, 1).start()
    w_pin.start()
    w_ids.start()
    acc[...] = jnp.zeros_like(acc)

    def expert_out(o, m, e0, count):
        esend[o - 1, m, pl.ds(e0 * qc, count * qc)] = jnp.dot(
            vea[o, m, pl.ds(e0, count)].reshape(count * qc, hidden), vepin[...], preferred_element_type=jnp.float32
        )

    half = max(experts // 2, 1)
    w_epin.wait()
    for o in range(1, nt):
        load_ea(o, 0, 1, 0).wait()
        expert_out(o, 0, 0, half)
    pl.semaphore_wait(barrier, nt - 1 + ne - 1 + stride - 1 + on_line)
    for o in range(1, nt):
        send_e(o, 0, 0, half).start()
    for l in range(layers):
        for o in range(1, nt):
            load_a(o, l).start()
    w_pout.start()
    next_line(0)
    if half < experts:
        for o in range(1, nt):
            expert_out(o, 0, half, experts - half)
            send_e(o, 0, half, experts - half).start()
    for o in range(1, nt):
        load_ea(o, 1, micro - 1, 1).wait()

    @pl.loop(1, micro)
    def _(m):
        for o in range(1, nt):
            expert_out(o, m, 0, experts)
            send_e(o, m, 0, experts).start()

    w_pin.wait()
    w_dval.start()
    hear_line(0)
    next_line(1)
    for l in range(layers):
        for o in range(1, nt):
            load_a(o, l).wait()
        load_a(0, l).start()
        load_c(l).start()
        if l == layers - 1:
            hear_line(1)
            next_line(2)

        @pl.loop(0, micro)
        def _(m):
            k = l * micro + m
            for o in range(1, nt):
                dsend[o - 1, pl.ds(pl.multiple_of(k * q, q), q)] = jnp.dot(
                    va[o, l, m], vpin[l], preferred_element_type=jnp.float32
                )
                for p in range(PIECES):
                    j = k * PIECES + p

                    @pl.when(j >= lent)
                    def _():
                        send_d(o, j).start()

    load_ea(0, 0, micro, 0).start()
    load_ec.start()
    hear_line(2)
    for r in range(3, line_rounds):
        next_line(r)
        hear_line(r)
    tell_row(row_sem)
    w_pout.wait()
    w_dval.wait()
    w_epout.start()
    w_eval.start()
    w_ids.wait()
    w_prior.start()

    lanes = rows.shape[2]
    lane = lax.broadcasted_iota(jnp.int32, (1, lanes), 1)

    def domain_of(m):
        return jnp.where(lane == vids[m], 1.0, 0.0)

    for j in range(LENT):
        mask[j] = domain_of(j // PIECES % micro)

    @pl.when(lent > 0)
    def _():
        lend_mask().start()
        for j in range(LENT):

            @pl.when(j < lent)
            def _():
                for o in range(1, nt):
                    lend_u(o, j).start()

    def fold(m, value):
        acc[m] += jnp.sum(value.reshape(-1, 8, rank), axis=0)

    for l in range(layers):
        load_a(0, l).wait()
        load_c(l).wait()
        if l == layers - 1:
            pl.semaphore_wait(row_sem, stride - 1)
            tell_tensor(tensor_sem)

        @pl.loop(0, micro)
        def _(m):
            k = l * micro + m
            u = jnp.dot(va[0, l, m], vpin[l], preferred_element_type=jnp.float32)
            w = jnp.dot(vc[l, m], vpout[l], preferred_element_type=jnp.float32)
            g = lax.dot_general(
                w, vdv[l], (((1,), (1,)), ((), ())), precision=HIGHEST, preferred_element_type=jnp.float32
            )
            dg[pl.ds(pl.multiple_of(k * q, q), q)] = g
            fold(m, u * g)
            if l * micro * PIECES < LENT:
                for p in range(PIECES):

                    @pl.when(k * PIECES + p < lent)
                    def _():
                        lend_g(k * PIECES + p).start()

    w_epout.wait()
    w_eval.wait()
    load_ea(0, 0, micro, 0).wait()
    load_ec.wait()
    pl.semaphore_wait(tensor_sem, nt - 1)

    @pl.loop(0, micro)
    def _(m):
        u = jnp.dot(vea[0, m].reshape(experts * qc, hidden), vepin[...], preferred_element_type=jnp.float32)
        w = jnp.dot(vec[m].reshape(experts * qc, dim), vepout[...], preferred_element_type=jnp.float32)
        g = jnp.concatenate(
            [
                lax.dot_general(
                    w[e * qc : (e + 1) * qc], vev[e], (((1,), (1,)), ((), ())),
                    precision=HIGHEST, preferred_element_type=jnp.float32,
                )
                for e in range(experts)
            ],
            axis=0,
        )
        eg[m] = g
        fold(m, u * g)

    landed(erecv, e_sem)

    @pl.loop(0, micro)
    def _(m):
        for o in range(1, nt):
            fold(m, erecv[o - 1, m] * eg[m])

    w_prior.wait()

    def cross(o, j):
        return drecv[o - 1, rows_of(j)] * dg[rows_of(j)]

    def total_of(value):
        return jnp.sum(jnp.sum(value, axis=1, keepdims=True), axis=0, keepdims=True)

    for j in range(LENT):

        @pl.when(j >= lent)
        def _():
            for o in range(1, nt):
                landed(drecv.at[o - 1, rows_of(j)], d_sem.at[o - 1, j])
                fold(j // PIECES % micro, cross(o, j))

    rows[me] = jnp.zeros((1, lanes), jnp.float32)

    @pl.when(taken > 0)
    def _():
        landed(lmask, lg_sem.at[LENT])
        for j in range(LENT):

            @pl.when(j < taken)
            def _():
                landed(lg.at[rows_of(j)], lg_sem.at[j])
                value = jnp.zeros((8, rank), jnp.float32)
                for o in range(1, nt):
                    landed(lu.at[o - 1, rows_of(j)], lu_sem.at[o - 1, j])
                    both = lu[o - 1, rows_of(j)] * lg[rows_of(j)]
                    value = value + jnp.sum(both.reshape(-1, 8, rank), axis=0)
                rows[me] += lmask[j] * total_of(value)

    for o in range(1, nt):
        landed(drecv.at[o - 1, rows_of(LENT, units - ALONE - LENT)], d_sem.at[o - 1, LENT])

    @pl.loop(LENT, units - ALONE)
    def _(j):
        for o in range(1, nt):
            fold(lax.rem(lax.div(j, PIECES), micro), cross(o, j))

    last = [(o, j) for j in range(units - ALONE, units) for o in range(1, nt)]
    for o, j in last[:-1]:
        landed(drecv.at[o - 1, rows_of(j)], d_sem.at[o - 1, j - units + ALONE + LENT + 1])
        fold(j // PIECES % micro, cross(o, j))

    part = rows[me]
    for m in range(micro):
        part = part + domain_of(m) * total_of(acc[m])
    rows[me] = part
    chosen = domain_of(micro - 1)
    o, j = last[-1]
    landed(drecv.at[o - 1, rows_of(j)], d_sem.at[o - 1, ALONE + LENT])
    rows[me] += chosen * total_of(jnp.sum(cross(o, j).reshape(-1, 8, rank), axis=0))

    for i in range(1, n):
        t = me + i
        pltpu.make_async_remote_copy(
            src_ref=rows.at[me], dst_ref=rows.at[me], send_sem=row_send, recv_sem=row_recv,
            device_id=jnp.where(t < n, t, t - n), device_id_type=LOGICAL,
        ).start()

    for o in range(1, nt):
        landed(dsend.at[o - 1], s_sem.at[0])
    landed(esend, s_sem.at[1])

    @pl.when(lent > 0)
    def _():
        lend_mask().wait_send()
        for j in range(LENT):

            @pl.when(j < lent)
            def _():
                lend_g(j).wait_send()

    others = rows.at[pl.ds(0, n - 1)]
    landed(others, row_recv)
    domains = prior.shape[1]
    total = jnp.sum(rows[...], axis=0)[:, :domains]
    spread = jnp.sqrt(jnp.sum(total * total, axis=1, keepdims=True) * (1.0 / domains) + 1e-06)
    z = total / spread
    mix = vprior[...]
    mass = jnp.sum(mix * jnp.exp(0.5 * z), axis=1, keepdims=True)
    out[...] = jnp.log(mix) + 0.5 * z - jnp.log(mass)
    landed(others, row_send)


def per_device(sizes, *args):
    (act, cot, pin, pout, eact, ecot, epin, epout, dval, evals, ids, prior) = args
    nd, ne, nt = sizes
    n = nd * ne * nt
    places = line_of(nd)[1]
    layers, micro, q, dim = cot.shape
    rank, feat = pin.shape[2], pin.shape[1]
    experts, qc, hidden = ecot.shape[1], ecot.shape[2], eact.shape[3]
    domains = prior.shape[0]
    lanes = -(-domains // 128) * 128
    lent = LENT * (q // PIECES)
    bf, f32 = jnp.bfloat16, jnp.float32
    V, dma, regular = pltpu.VMEM, pltpu.SemaphoreType.DMA, pltpu.SemaphoreType.REGULAR
    logs = pl.pallas_call(
        functools.partial(kernel, sizes),
        out_shape=pltpu.VMEM((1, domains), f32),
        in_specs=[pl.BlockSpec(memory_space=pltpu.HBM)] * 12,
        out_specs=pl.BlockSpec(memory_space=pltpu.VMEM),
        scratch_shapes=[
            V((nt, layers, micro, q, feat), bf),
            V((layers, micro, q, dim), bf),
            V(pin.shape, bf),
            V(pout.shape, bf),
            V((nt, micro, experts, qc, hidden), bf),
            V((micro, experts, qc, dim), bf),
            V(epin.shape, bf),
            V(epout.shape, bf),
            V(dval.shape, f32),
            V(evals.shape, f32),
            pltpu.SMEM(ids.shape, jnp.int32),
            V((1, domains), f32),
            V((nt - 1, layers * micro * q, rank), f32),
            V((nt - 1, layers * micro * q, rank), f32),
            V((nt - 1, micro, experts * qc, rank), f32),
            V((nt - 1, micro, experts * qc, rank), f32),
            V((layers * micro * q, rank), f32),
            V((micro, experts * qc, rank), f32),
            V((nt - 1, lent, rank), f32),
            V((lent, rank), f32),
            V((LENT, 1, lanes), f32),
            V((LENT, 1, lanes), f32),
            V((micro, 8, rank), f32),
            V((n, 1, lanes), f32),
            dma((layers,)),
            dma((layers,)),
            dma((2,)),
            dma((3,)),
            dma((2,)),
            dma,
            dma((nt - 1, LENT + 1 + ALONE)),
            dma((nt - 1, LENT)),
            dma((LENT + 1,)),
            dma((LENT + 1,)),
            dma,
            dma,
            regular((max(places - 1, 1),)),
            regular,
            regular,
        ],
        compiler_params=pltpu.CompilerParams(
            collective_id=0, has_side_effects=True, vmem_limit_bytes=60 * 1024 * 1024
        ),
        name="align",
    )(act, cot, pin, pout, eact, ecot, epin, epout, dval, evals, ids, prior.reshape(1, domains))
    share = domains // nd
    return lax.dynamic_slice_in_dim(logs[0], lax.axis_index("dp") * share, share, 0)


def solution(mesh):
    sizes = (mesh.shape["dp"], mesh.shape["expert"], mesh.shape["tensor"])
    placed = (
        P(None, "dp", "expert", "tensor"),
        P(None, "dp", ("expert", "tensor"), None),
        P(None, "tensor", None),
        P(),
        P("dp", "expert", None, "tensor"),
        P("dp", "expert", "tensor", None),
        P("tensor", None),
        P(),
        P(),
        P("expert", None, None),
        P("dp"),
        P(),
    )
    return jax.shard_map(
        functools.partial(per_device, sizes), mesh=mesh, in_specs=placed, out_specs=P("dp"), check_vma=False
    )
```

time: 30.7 us -> 28.5 us (0.928)
  Pallas kernels: 29.9 us -> 27.8 us
    pallas_call x1, Pallas kernels: 29.9 us -> 27.8 us  [per_device(): pl.pallas_call(functools.partial(kernel, sizes), out_shape=pltpu.VMEM((1,...]
where the time goes in v2:
time: 28.5 us; the launch traced here: 28.4 us
  Pallas kernels  27.8 us (98%)
  local copies, waits for them, and re-layouts  0.59 us (2%)
    pallas_call x1, Pallas kernels, per_device(): pl.pallas_call(functools.partial(kernel, sizes), out_shape=pltpu.VMEM((1,...  27.8 us
    dynamic_slice x1, local copies, waits for them, and re-layouts, per_device(): lax.dynamic_slice_in_dim(logs[0], lax.axis_index('dp') * share, share, 0)  0.59 us

profile of v2, /device:TPU:0, one launch (start us, length us, event | category | flops | bytes accessed | tf_op | source)
XLA Modules:
  0.0 28.4 jit_solution(2598578133180710585)
XLA Ops:
  0.0 27.8 %align.1 = f32[1,64]{1,0:T(1,128)S(1)} custom-call(bf16[2,4,256,1792]{3,2,1,0:T(8,128)(2,1)} %act.1, bf16[2,4,128,3584]{3,2,1,0:T(8,128)(2,1)} %cot.1, bf16[2,1792,128]{2,1,0:T(8,128)(2,1)} %pin.1, bf16[2,3584,128]{2,1,0:T(8,128)(2,1)} %pout.1, bf16[4,4,64,1280]{3,2,1,0:T(8,128)(2,1)} %eact.1, bf16[4,4,32,3584]{3,2,1,0:T(8,128)(2,1)} %ecot.1, ...), custom_call_target="tpu_custom_call" | custom-call | tf_op jit(solution)/shard_map/align/pallas_call | solution.py:419
  27.8 0.6 %dynamic-slice_bitcast_fusion = f32[8]{0:T(128)} fusion(f32[1,64]{1,0:T(1,128)S(1)} %align.1, s32[]{:T(128)S(6)} %select_n.3), kind=kLoop, calls=%fused_computation | loop fusion | bytes 68 | tf_op jit(solution)/shard_map/dynamic_slice | solution.py:471

commit v3 on v2

--- a/solution.py
+++ b/solution.py
@@ -9,9 +9,13 @@
 
 MESH, LOGICAL = pl.DeviceIdType.MESH, pl.DeviceIdType.LOGICAL
 HIGHEST = lax.Precision.HIGHEST
+BATCH = 2
 PIECES = 2
 LENT = 3
-ALONE = 4
+GIVEN = 2
+ACROSS = LENT + GIVEN
+CROWD = ACROSS + 1
+ALONE = 3
 
 
 def line_of(nd):
@@ -24,8 +28,8 @@
     act, cot, pin, pout, eact, ecot, epin, epout, dval, evals, ids, prior,
     out,
     va, vc, vpin, vpout, vea, vec, vepin, vepout, vdv, vev, vids, vprior,
-    dsend, drecv, esend, erecv, dg, eg, lu, lg, lmask, mask, acc, rows,
-    a_sem, c_sem, ea_sem, w_sem, s_sem, e_sem, d_sem, lu_sem, lg_sem, lg_send, row_send, row_recv,
+    dsend, drecv, esend, erecv, dg, eg, lu, lg, lmask, mask, ru, hu, hg, yru, yhu, yhg, ymask, acc, fin, rows,
+    a_sem, c_sem, ea_sem, w_sem, s_sem, e_sem, d_sem, l_sem, lg_send, r_sem, hu_sem, r_send, y_sem, y_send, row_send, row_recv,
     line_sem, row_sem, tensor_sem,
 ):
     nd, ne, nt = sizes
@@ -41,12 +45,16 @@
     h = q // PIECES
     blocks = layers * micro
     units = blocks * PIECES
+    batch = BATCH if micro % BATCH == 0 else 1
     mate = (places - 1 - place) * stride + row
 
     def lends(at):
-        return jnp.where(2 * at >= places, jnp.clip(2 * (at + row - (places + stride) // 2 + 1) - 1, 0, LENT), 0)
+        return jnp.where(2 * at >= places, jnp.clip(2 * (at + row - (places + stride) // 2 + 1) - row, 0, LENT), 0)
 
     lent, taken = lends(place), lends(places - 1 - place)
+    near = 2 * place < places
+    over, guest = ((row == 1) & near, (row == 0) & near) if stride > 1 else (row < 0, row < 0)
+    giver, helper = (ex == 0, ex == 1) if ne > 1 else (ex < 0, ex < 0)
 
     def device(d=None, e=None, t=None):
         return {
@@ -83,7 +91,9 @@
         return lax.rem(tx + o, nt)
 
     def send_d(o, j):
-        i = jnp.minimum(j, LENT) + jnp.maximum(j - (units - ALONE - 1), 0)
+        i = jnp.maximum(j - (units - ALONE - 1), 0)
+        for first in (LENT, ACROSS, CROWD):
+            i = i + jnp.where(j >= first, 1, 0)
         return pltpu.make_async_remote_copy(
             src_ref=dsend.at[o - 1, rows_of(j)], dst_ref=drecv.at[o - 1, rows_of(j)],
             send_sem=s_sem.at[0], recv_sem=d_sem.at[o - 1, i],
@@ -93,22 +103,71 @@
     def lend_u(o, j):
         return pltpu.make_async_remote_copy(
             src_ref=dsend.at[o - 1, rows_of(j)], dst_ref=lu.at[o - 1, rows_of(j)],
-            send_sem=s_sem.at[0], recv_sem=lu_sem.at[o - 1, j],
+            send_sem=s_sem.at[0], recv_sem=l_sem.at[1 + o],
             device_id=device(d=mate, t=opposite(o)), device_id_type=MESH,
         )
 
     def lend_g(j):
         return pltpu.make_async_remote_copy(
             src_ref=dg.at[rows_of(j)], dst_ref=lg.at[rows_of(j)],
-            send_sem=lg_send.at[j], recv_sem=lg_sem.at[j],
+            send_sem=lg_send.at[0], recv_sem=l_sem.at[0],
             device_id=device(d=mate), device_id_type=MESH,
         )
 
     def lend_mask():
         return pltpu.make_async_remote_copy(
-            src_ref=mask, dst_ref=lmask,
-            send_sem=lg_send.at[LENT], recv_sem=lg_sem.at[LENT],
+            src_ref=mask.at[pl.ds(0, LENT)], dst_ref=lmask,
+            send_sem=lg_send.at[1], recv_sem=l_sem.at[1],
             device_id=device(d=mate), device_id_type=MESH,
+        )
+
+    given = rows_of(LENT, GIVEN)
+
+    def give_u(o):
+        return pltpu.make_async_remote_copy(
+            src_ref=dsend.at[o - 1, given], dst_ref=ru.at[o - 1],
+            send_sem=s_sem.at[0], recv_sem=r_sem.at[o],
+            device_id=device(e=1), device_id_type=MESH,
+        )
+
+    def give_g():
+        return pltpu.make_async_remote_copy(
+            src_ref=dg.at[given], dst_ref=hg,
+            send_sem=lg_send.at[2], recv_sem=r_sem.at[0],
+            device_id=device(e=1), device_id_type=MESH,
+        )
+
+    def pass_on(o, i):
+        return pltpu.make_async_remote_copy(
+            src_ref=ru.at[o - 1, rows_of(i)], dst_ref=hu.at[o - 1, rows_of(i)],
+            send_sem=r_send, recv_sem=hu_sem.at[o - 1, i],
+            device_id=device(t=opposite(o)), device_id_type=MESH,
+        )
+
+    def pass_over_u(o):
+        return pltpu.make_async_remote_copy(
+            src_ref=dsend.at[o - 1, rows_of(ACROSS)], dst_ref=yru.at[o - 1],
+            send_sem=s_sem.at[0], recv_sem=y_sem.at[1 + o],
+            device_id=device(d=place * stride), device_id_type=MESH,
+        )
+
+    def pass_over_g():
+        return pltpu.make_async_remote_copy(
+            src_ref=dg.at[rows_of(ACROSS)], dst_ref=yhg, send_sem=y_send.at[0], recv_sem=y_sem.at[0],
+            device_id=device(d=place * stride), device_id_type=MESH,
+        )
+
+    def pass_over_mask():
+        return pltpu.make_async_remote_copy(
+            src_ref=mask.at[LENT], dst_ref=ymask, send_sem=y_send.at[1], recv_sem=y_sem.at[1],
+            device_id=device(d=place * stride), device_id_type=MESH,
+        )
+
+    def pass_through(o):
+        return pltpu.make_async_remote_copy(
+            src_ref=yru.at[o - 1], dst_ref=yhu.at[o - 1],
+            send_sem=y_send.at[1 + o], recv_sem=y_sem.at[nt + o],
+            device_id=device(t=opposite(o)), device_id_type=MESH,
         )
 
     def send_e(o, m, e0, count):
@@ -212,22 +271,37 @@
             hear_line(1)
             next_line(2)
 
-        @pl.loop(0, micro)
-        def _(m):
-            k = l * micro + m
+        for first in range(0, micro, batch):
             for o in range(1, nt):
-                dsend[o - 1, pl.ds(pl.multiple_of(k * q, q), q)] = jnp.dot(
-                    va[o, l, m], vpin[l], preferred_element_type=jnp.float32
+                dsend[o - 1, pl.ds((l * micro + first) * q, batch * q)] = jnp.dot(
+                    va[o, l, first : first + batch].reshape(batch * q, pin.shape[1]), vpin[l],
+                    preferred_element_type=jnp.float32,
                 )
-                for p in range(PIECES):
-                    j = k * PIECES + p
-
-                    @pl.when(j >= lent)
+
+            @pl.loop(0, batch * PIECES)
+            def _(i):
+                j = (l * micro + first) * PIECES + i
+                for o in range(1, nt):
+                    kept = (giver & (j >= LENT) & (j < ACROSS)) | (over & (j == ACROSS))
+
+                    @pl.when((j >= lent) & ~kept)
                     def _():
                         send_d(o, j).start()
 
+                    @pl.when(giver & (j == ACROSS - 1))
+                    def _():
+                        give_u(o).start()
+
     load_ea(0, 0, micro, 0).start()
     load_ec.start()
+
+    @pl.when(helper)
+    def _():
+        for o in range(1, nt):
+            landed(ru.at[o - 1], r_sem.at[o])
+            for i in range(GIVEN):
+                pass_on(o, i).start()
+
     hear_line(2)
     for r in range(3, line_rounds):
         next_line(r)
@@ -248,6 +322,7 @@
 
     for j in range(LENT):
         mask[j] = domain_of(j // PIECES % micro)
+    mask[LENT] = domain_of(ACROSS // PIECES % micro)
 
     @pl.when(lent > 0)
     def _():
@@ -259,8 +334,17 @@
                 for o in range(1, nt):
                     lend_u(o, j).start()
 
+    @pl.when(over)
+    def _():
+        pass_over_mask().start()
+        for o in range(1, nt):
+            pass_over_u(o).start()
+
     def fold(m, value):
         acc[m] += jnp.sum(value.reshape(-1, 8, rank), axis=0)
+
+    def folds(some, value):
+        acc[some] += jnp.sum(value.reshape(batch, -1, 8, rank), axis=1)
 
     for l in range(layers):
         load_a(0, l).wait()
@@ -269,22 +353,36 @@
             pl.semaphore_wait(row_sem, stride - 1)
             tell_tensor(tensor_sem)
 
-        @pl.loop(0, micro)
-        def _(m):
-            k = l * micro + m
-            u = jnp.dot(va[0, l, m], vpin[l], preferred_element_type=jnp.float32)
-            w = jnp.dot(vc[l, m], vpout[l], preferred_element_type=jnp.float32)
+        for first in range(0, micro, batch):
+            some = slice(first, first + batch)
+            u = jnp.dot(
+                va[0, l, some].reshape(batch * q, pin.shape[1]), vpin[l], preferred_element_type=jnp.float32
+            )
+            w = jnp.dot(vc[l, some].reshape(batch * q, dim), vpout[l], preferred_element_type=jnp.float32)
             g = lax.dot_general(
                 w, vdv[l], (((1,), (1,)), ((), ())), precision=HIGHEST, preferred_element_type=jnp.float32
             )
-            dg[pl.ds(pl.multiple_of(k * q, q), q)] = g
-            fold(m, u * g)
-            if l * micro * PIECES < LENT:
-                for p in range(PIECES):
-
-                    @pl.when(k * PIECES + p < lent)
+            dg[pl.ds((l * micro + first) * q, batch * q)] = g
+            folds(some, u * g)
+            done = range((l * micro + first) * PIECES, (l * micro + first + batch) * PIECES)
+            for j in range(LENT):
+                if j in done:
+
+                    @pl.when(j < lent)
                     def _():
-                        lend_g(k * PIECES + p).start()
+                        lend_g(j).start()
+
+            if ACROSS - 1 in done:
+
+                @pl.when(giver)
+                def _():
+                    give_g().start()
+
+            if ACROSS in done:
+
+                @pl.when(over)
+                def _():
+                    pass_over_g().start()
 
     w_epout.wait()
     w_eval.wait()
@@ -292,27 +390,35 @@
     load_ec.wait()
     pl.semaphore_wait(tensor_sem, nt - 1)
 
+    for first in range(0, micro, batch):
+        some = slice(first, first + batch)
+        u = jnp.dot(
+            vea[0, some].reshape(batch * experts * qc, hidden), vepin[...], preferred_element_type=jnp.float32
+        )
+        w = jnp.dot(vec[some].reshape(batch * experts * qc, dim), vepout[...], preferred_element_type=jnp.float32)
+        w = w.reshape(batch, experts, qc, rank)
+        g = [
+            lax.dot_general(
+                w[:, e].reshape(batch * qc, rank), vev[e], (((1,), (1,)), ((), ())),
+                precision=HIGHEST, preferred_element_type=jnp.float32,
+            ).reshape(batch, 1, qc, rank)
+            for e in range(experts)
+        ]
+        g = jnp.concatenate(g, axis=1).reshape(batch, experts * qc, rank)
+        eg[some] = g
+        folds(some, u.reshape(batch, experts * qc, rank) * g)
+        if first == 0:
+
+            @pl.when(guest)
+            def _():
+                for o in range(1, nt):
+                    landed(yru.at[o - 1], y_sem.at[1 + o])
+                    pass_through(o).start()
+
+    landed(erecv, e_sem)
+
     @pl.loop(0, micro)
     def _(m):
-        u = jnp.dot(vea[0, m].reshape(experts * qc, hidden), vepin[...], preferred_element_type=jnp.float32)
-        w = jnp.dot(vec[m].reshape(experts * qc, dim), vepout[...], preferred_element_type=jnp.float32)
-        g = jnp.concatenate(
-            [
-                lax.dot_general(
-                    w[e * qc : (e + 1) * qc], vev[e], (((1,), (1,)), ((), ())),
-                    precision=HIGHEST, preferred_element_type=jnp.float32,
-                )
-                for e in range(experts)
-            ],
-            axis=0,
-        )
-        eg[m] = g
-        fold(m, u * g)
-
-    landed(erecv, e_sem)
-
-    @pl.loop(0, micro)
-    def _(m):
         for o in range(1, nt):
             fold(m, erecv[o - 1, m] * eg[m])
 
@@ -324,58 +430,116 @@
     def total_of(value):
         return jnp.sum(jnp.sum(value, axis=1, keepdims=True), axis=0, keepdims=True)
 
-    for j in range(LENT):
-
-        @pl.when(j >= lent)
+    for c in range(LENT):
+
+        @pl.when(lent == c)
         def _():
             for o in range(1, nt):
-                landed(drecv.at[o - 1, rows_of(j)], d_sem.at[o - 1, j])
-                fold(j // PIECES % micro, cross(o, j))
+                landed(drecv.at[o - 1, rows_of(c, LENT - c)], d_sem.at[o - 1, 0])
+                for j in range(c, LENT):
+                    fold(j // PIECES % micro, cross(o, j))
 
     rows[me] = jnp.zeros((1, lanes), jnp.float32)
 
     @pl.when(taken > 0)
     def _():
-        landed(lmask, lg_sem.at[LENT])
+        landed(lmask, l_sem.at[1])
+        for c in range(1, LENT + 1):
+
+            @pl.when(taken == c)
+            def _():
+                landed(lg.at[rows_of(0, c)], l_sem.at[0])
+                for o in range(1, nt):
+                    landed(lu.at[o - 1, rows_of(0, c)], l_sem.at[1 + o])
+
         for j in range(LENT):
 
             @pl.when(j < taken)
             def _():
-                landed(lg.at[rows_of(j)], lg_sem.at[j])
                 value = jnp.zeros((8, rank), jnp.float32)
                 for o in range(1, nt):
-                    landed(lu.at[o - 1, rows_of(j)], lu_sem.at[o - 1, j])
                     both = lu[o - 1, rows_of(j)] * lg[rows_of(j)]
                     value = value + jnp.sum(both.reshape(-1, 8, rank), axis=0)
                 rows[me] += lmask[j] * total_of(value)
 
+    @pl.when(~giver)
+    def _():
+        for o in range(1, nt):
+            landed(drecv.at[o - 1, given], d_sem.at[o - 1, 1])
+            for j in range(LENT, ACROSS):
+                fold(j // PIECES % micro, cross(o, j))
+
+    @pl.when(~over)
+    def _():
+        for o in range(1, nt):
+            landed(drecv.at[o - 1, rows_of(ACROSS)], d_sem.at[o - 1, 2])
+            fold(ACROSS // PIECES % micro, cross(o, ACROSS))
+
     for o in range(1, nt):
-        landed(drecv.at[o - 1, rows_of(LENT, units - ALONE - LENT)], d_sem.at[o - 1, LENT])
-
-    @pl.loop(LENT, units - ALONE)
+        landed(drecv.at[o - 1, rows_of(CROWD, units - ALONE - CROWD)], d_sem.at[o - 1, 3])
+
+    @pl.loop(CROWD, units - ALONE)
     def _(j):
         for o in range(1, nt):
             fold(lax.rem(lax.div(j, PIECES), micro), cross(o, j))
+
+    def take(o, j):
+        landed(drecv.at[o - 1, rows_of(j)], d_sem.at[o - 1, j - units + ALONE + 4])
+
+    def take_given(o, i):
+        landed(hu.at[o - 1, rows_of(i)], hu_sem.at[o - 1, i])
+        return hu[o - 1, rows_of(i)] * hg[rows_of(i)]
+
+    def shorter(value):
+        return jnp.sum(value.reshape(-1, 8, rank), axis=0)
 
     last = [(o, j) for j in range(units - ALONE, units) for o in range(1, nt)]
     for o, j in last[:-1]:
-        landed(drecv.at[o - 1, rows_of(j)], d_sem.at[o - 1, j - units + ALONE + LENT + 1])
+        take(o, j)
         fold(j // PIECES % micro, cross(o, j))
+    o, j = last[-1]
+
+    @pl.when(guest)
+    def _():
+        landed(ymask, y_sem.at[1])
+        landed(yhg, y_sem.at[0])
+        value = jnp.zeros((8, rank), jnp.float32)
+        for o_ in range(1, nt):
+            landed(yhu.at[o_ - 1], y_sem.at[nt + o_])
+            value = value + shorter(yhu[o_ - 1] * yhg[...])
+        rows[me] += ymask[...] * total_of(value)
+
+    @pl.when(helper)
+    def _():
+        take(o, j)
+        fold(micro - 1, cross(o, j))
+        landed(hg, r_sem.at[0])
+        for i in range(GIVEN):
+            for o_ in range(1, nt):
+                if (i, o_) != (GIVEN - 1, nt - 1):
+                    fold((LENT + i) // PIECES % micro, take_given(o_, i))
 
     part = rows[me]
     for m in range(micro):
         part = part + domain_of(m) * total_of(acc[m])
     rows[me] = part
-    chosen = domain_of(micro - 1)
-    o, j = last[-1]
-    landed(drecv.at[o - 1, rows_of(j)], d_sem.at[o - 1, ALONE + LENT])
-    rows[me] += chosen * total_of(jnp.sum(cross(o, j).reshape(-1, 8, rank), axis=0))
-
-    for i in range(1, n):
-        t = me + i
+    chosen = jnp.where(helper, domain_of((ACROSS - 1) // PIECES % micro), domain_of(micro - 1))
+
+    @pl.when(helper)
+    def _():
+        fin[...] = shorter(take_given(nt - 1, GIVEN - 1))
+
+    @pl.when(~helper)
+    def _():
+        take(o, j)
+        fin[...] = shorter(cross(o, j))
+
+    rows[me] += chosen * total_of(fin[...])
+
+    for i in range(n - 1):
         pltpu.make_async_remote_copy(
             src_ref=rows.at[me], dst_ref=rows.at[me], send_sem=row_send, recv_sem=row_recv,
-            device_id=jnp.where(t < n, t, t - n), device_id_type=LOGICAL,
+            device_id=i + (me <= i).astype(jnp.int32), device_id_type=LOGICAL,
         ).start()
 
     for o in range(1, nt):
@@ -385,11 +549,28 @@
     @pl.when(lent > 0)
     def _():
         lend_mask().wait_send()
-        for j in range(LENT):
-
-            @pl.when(j < lent)
+        for c in range(1, LENT + 1):
+
+            @pl.when(lent == c)
             def _():
-                lend_g(j).wait_send()
+                landed(dg.at[rows_of(0, c)], lg_send.at[0])
+
+    @pl.when(giver)
+    def _():
+        give_g().wait_send()
+
+    @pl.when(helper)
+    def _():
+        landed(ru, r_send)
+    @pl.when(over)
+    def _():
+        pass_over_mask().wait_send()
+        pass_over_g().wait_send()
+
+    @pl.when(guest)
+    def _():
+        for o in range(1, nt):
+            pass_through(o).wait_send()
 
     others = rows.at[pl.ds(0, n - 1)]
     landed(others, row_recv)
@@ -413,7 +594,7 @@
     experts, qc, hidden = ecot.shape[1], ecot.shape[2], eact.shape[3]
     domains = prior.shape[0]
     lanes = -(-domains // 128) * 128
-    lent = LENT * (q // PIECES)
+    lent, given = LENT * (q // PIECES), GIVEN * (q // PIECES)
     bf, f32 = jnp.bfloat16, jnp.float32
     V, dma, regular = pltpu.VMEM, pltpu.SemaphoreType.DMA, pltpu.SemaphoreType.REGULAR
     logs = pl.pallas_call(
@@ -443,8 +624,16 @@
             V((nt - 1, lent, rank), f32),
             V((lent, rank), f32),
             V((LENT, 1, lanes), f32),
-            V((LENT, 1, lanes), f32),
+            V((LENT + 1, 1, lanes), f32),
+            V((nt - 1, given, rank), f32),
+            V((nt - 1, given, rank), f32),
+            V((given, rank), f32),
+            V((nt - 1, q // PIECES, rank), f32),
+            V((nt - 1, q // PIECES, rank), f32),
+            V((q // PIECES, rank), f32),
+            V((1, lanes), f32),
             V((micro, 8, rank), f32),
+            V((8, rank), f32),
             V((n, 1, lanes), f32),
             dma((layers,)),
             dma((layers,)),
@@ -452,10 +641,14 @@
             dma((3,)),
             dma((2,)),
             dma,
-            dma((nt - 1, LENT + 1 + ALONE)),
-            dma((nt - 1, LENT)),
-            dma((LENT + 1,)),
-            dma((LENT + 1,)),
+            dma((nt - 1, 4 + ALONE)),
+            dma((1 + nt,)),
+            dma((3,)),
+            dma((nt,)),
+            dma((nt - 1, GIVEN)),
+            dma,
+            dma((2 * nt,)),
+            dma((1 + nt,)),
             dma,
             dma,
             regular((max(places - 1, 1),)),

time: 28.5 us -> 27.4 us (0.961)
  Pallas kernels: 27.8 us -> 26.7 us
    pallas_call x1, Pallas kernels: 27.8 us -> 26.7 us  [per_device(): pl.pallas_call(functools.partial(kernel, sizes), out_shape=pltpu.VMEM((1,...]
where the time goes in v3:
time: 27.4 us; the launch traced here: 27.3 us
  Pallas kernels  26.7 us (97%)
  local copies, waits for them, and re-layouts  0.59 us (2%)
    pallas_call x1, Pallas kernels, per_device(): pl.pallas_call(functools.partial(kernel, sizes), out_shape=pltpu.VMEM((1,...  26.7 us
    dynamic_slice x1, local copies, waits for them, and re-layouts, per_device(): lax.dynamic_slice_in_dim(logs[0], lax.axis_index('dp') * share, share, 0)  0.59 us

profile of v3, /device:TPU:0, one launch (start us, length us, event | category | flops | bytes accessed | tf_op | source)
XLA Modules:
  0.0 27.3 jit_solution(2282442569486687601)
XLA Ops:
  0.0 26.7 %align.1 = f32[1,64]{1,0:T(1,128)S(1)} custom-call(bf16[2,4,256,1792]{3,2,1,0:T(8,128)(2,1)} %act.1, bf16[2,4,128,3584]{3,2,1,0:T(8,128)(2,1)} %cot.1, bf16[2,1792,128]{2,1,0:T(8,128)(2,1)} %pin.1, bf16[2,3584,128]{2,1,0:T(8,128)(2,1)} %pout.1, bf16[4,4,64,1280]{3,2,1,0:T(8,128)(2,1)} %eact.1, bf16[4,4,32,3584]{3,2,1,0:T(8,128)(2,1)} %ecot.1, ...), custom_call_target="tpu_custom_call" | custom-call | tf_op jit(solution)/shard_map/align/pallas_call | solution.py:600
  26.7 0.6 %dynamic-slice_bitcast_fusion = f32[8]{0:T(128)} fusion(f32[1,64]{1,0:T(1,128)S(1)} %align.1, s32[]{:T(128)S(6)} %select_n.3), kind=kLoop, calls=%fused_computation | loop fusion | bytes 68 | tf_op jit(solution)/shard_map/dynamic_slice | solution.py:664

commit v4 on v3

--- a/solution.py
+++ b/solution.py
@@ -10,12 +10,13 @@
 MESH, LOGICAL = pl.DeviceIdType.MESH, pl.DeviceIdType.LOGICAL
 HIGHEST = lax.Precision.HIGHEST
 BATCH = 2
-PIECES = 2
-LENT = 3
-GIVEN = 2
-ACROSS = LENT + GIVEN
-CROWD = ACROSS + 1
-ALONE = 3
+PIECES = 4
+LENT = 5
+GIVEN = 6
+OVER = 2
+FIRST = LENT + GIVEN
+CROWD = FIRST + OVER
+ALONE = 2
 
 
 def line_of(nd):
@@ -28,8 +29,8 @@
     act, cot, pin, pout, eact, ecot, epin, epout, dval, evals, ids, prior,
     out,
     va, vc, vpin, vpout, vea, vec, vepin, vepout, vdv, vev, vids, vprior,
-    dsend, drecv, esend, erecv, dg, eg, lu, lg, lmask, mask, ru, hu, hg, yru, yhu, yhg, ymask, acc, fin, rows,
-    a_sem, c_sem, ea_sem, w_sem, s_sem, e_sem, d_sem, l_sem, lg_send, r_sem, hu_sem, r_send, y_sem, y_send, row_send, row_recv,
+    dsend, drecv, esend, erecv, dg, eg, lu, lg, lmask, mask, ru, hu, hg, yru, yhu, yhg, acc, fin, rows,
+    a_sem, ea_sem, w_sem, s_sem, e_sem, d_sem, l_sem, u_send, r_sem, hu_sem, y_sem, row_send, row_recv,
     line_sem, row_sem, tensor_sem,
 ):
     nd, ne, nt = sizes
@@ -49,12 +50,18 @@
     mate = (places - 1 - place) * stride + row
 
     def lends(at):
-        return jnp.where(2 * at >= places, jnp.clip(2 * (at + row - (places + stride) // 2 + 1) - row, 0, LENT), 0)
+        return jnp.where(2 * at >= places, jnp.clip(3 * (at + row - (places + stride) // 2 + 1) - row, 0, LENT), 0)
 
     lent, taken = lends(place), lends(places - 1 - place)
     near = 2 * place < places
     over, guest = ((row == 1) & near, (row == 0) & near) if stride > 1 else (row < 0, row < 0)
     giver, helper = (ex == 0, ex == 1) if ne > 1 else (ex < 0, ex < 0)
+
+    def kept(j):
+        return (j < lent) | (giver & (j >= LENT) & (j < FIRST)) | (over & (j >= FIRST) & (j < CROWD))
+
+    def count_of(flag):
+        return jnp.where(flag, 1, 0)
 
     def device(d=None, e=None, t=None):
         return {
@@ -65,7 +72,7 @@
 
     def load_a(o, l):
         first = pl.multiple_of(lax.rem(tx + o, nt) * q, q)
-        return pltpu.make_async_copy(act.at[l, :, pl.ds(first, q), :], va.at[o, l], a_sem.at[l])
+        return pltpu.make_async_copy(act.at[l, :, pl.ds(first, q), :], va.at[o * layers + l], a_sem.at[l])
 
     def load_ea(o, first_m, count, i):
         first = pl.multiple_of(lax.rem(tx + o, nt) * qc, qc)
@@ -73,7 +80,7 @@
         return pltpu.make_async_copy(eact.at[some, :, pl.ds(first, qc), :], vea.at[o, some], ea_sem.at[i])
 
     def load_c(l):
-        return pltpu.make_async_copy(cot.at[l], vc.at[l], c_sem.at[l])
+        return pltpu.make_async_copy(cot.at[l], vc.at[l], a_sem.at[l])
 
     load_ec = pltpu.make_async_copy(ecot, vec, ea_sem.at[1])
 
@@ -82,7 +89,7 @@
 
     w_epin, w_pout, w_epout = load_w(epin, vepin, 0), load_w(pout, vpout, 0), load_w(epout, vepout, 0)
     w_pin, w_dval, w_eval = load_w(pin, vpin, 1), load_w(dval, vdv, 1), load_w(evals, vev, 1)
-    w_ids, w_prior = load_w(ids, vids, 2), load_w(prior, vprior, 2)
+    w_ids, w_prior = pltpu.make_async_copy(ids, vids, ea_sem.at[0]), load_w(prior, vprior, 0)
 
     def rows_of(j, count=1):
         return pl.ds(pl.multiple_of(j * h, h), count * h)
@@ -92,8 +99,6 @@
 
     def send_d(o, j):
         i = jnp.maximum(j - (units - ALONE - 1), 0)
-        for first in (LENT, ACROSS, CROWD):
-            i = i + jnp.where(j >= first, 1, 0)
         return pltpu.make_async_remote_copy(
             src_ref=dsend.at[o - 1, rows_of(j)], dst_ref=drecv.at[o - 1, rows_of(j)],
             send_sem=s_sem.at[0], recv_sem=d_sem.at[o - 1, i],
@@ -103,21 +108,21 @@
     def lend_u(o, j):
         return pltpu.make_async_remote_copy(
             src_ref=dsend.at[o - 1, rows_of(j)], dst_ref=lu.at[o - 1, rows_of(j)],
-            send_sem=s_sem.at[0], recv_sem=l_sem.at[1 + o],
+            send_sem=s_sem.at[0], recv_sem=l_sem.at[0],
             device_id=device(d=mate, t=opposite(o)), device_id_type=MESH,
         )
 
     def lend_g(j):
         return pltpu.make_async_remote_copy(
             src_ref=dg.at[rows_of(j)], dst_ref=lg.at[rows_of(j)],
-            send_sem=lg_send.at[0], recv_sem=l_sem.at[0],
+            send_sem=u_send.at[0], recv_sem=l_sem.at[0],
             device_id=device(d=mate), device_id_type=MESH,
         )
 
     def lend_mask():
         return pltpu.make_async_remote_copy(
-            src_ref=mask.at[pl.ds(0, LENT)], dst_ref=lmask,
-            send_sem=lg_send.at[1], recv_sem=l_sem.at[1],
+            src_ref=mask, dst_ref=lmask.at[0],
+            send_sem=u_send.at[1], recv_sem=l_sem.at[2],
             device_id=device(d=mate), device_id_type=MESH,
         )
 
@@ -133,40 +138,40 @@
     def give_g():
         return pltpu.make_async_remote_copy(
             src_ref=dg.at[given], dst_ref=hg,
-            send_sem=lg_send.at[2], recv_sem=r_sem.at[0],
+            send_sem=u_send.at[0], recv_sem=r_sem.at[0],
             device_id=device(e=1), device_id_type=MESH,
         )
 
     def pass_on(o, i):
         return pltpu.make_async_remote_copy(
             src_ref=ru.at[o - 1, rows_of(i)], dst_ref=hu.at[o - 1, rows_of(i)],
-            send_sem=r_send, recv_sem=hu_sem.at[o - 1, i],
+            send_sem=u_send.at[0], recv_sem=hu_sem.at[o - 1, i // (GIVEN - 1)],
             device_id=device(t=opposite(o)), device_id_type=MESH,
         )
 
     def pass_over_u(o):
         return pltpu.make_async_remote_copy(
-            src_ref=dsend.at[o - 1, rows_of(ACROSS)], dst_ref=yru.at[o - 1],
-            send_sem=s_sem.at[0], recv_sem=y_sem.at[1 + o],
+            src_ref=dsend.at[o - 1, rows_of(FIRST, OVER)], dst_ref=yru.at[o - 1],
+            send_sem=s_sem.at[0], recv_sem=y_sem.at[o - 1],
             device_id=device(d=place * stride), device_id_type=MESH,
         )
 
     def pass_over_g():
         return pltpu.make_async_remote_copy(
-            src_ref=dg.at[rows_of(ACROSS)], dst_ref=yhg, send_sem=y_send.at[0], recv_sem=y_sem.at[0],
+            src_ref=dg.at[rows_of(FIRST, OVER)], dst_ref=yhg, send_sem=u_send.at[0], recv_sem=l_sem.at[1],
             device_id=device(d=place * stride), device_id_type=MESH,
         )
 
     def pass_over_mask():
         return pltpu.make_async_remote_copy(
-            src_ref=mask.at[LENT], dst_ref=ymask, send_sem=y_send.at[1], recv_sem=y_sem.at[1],
+            src_ref=mask, dst_ref=lmask.at[1], send_sem=u_send.at[1], recv_sem=l_sem.at[2],
             device_id=device(d=place * stride), device_id_type=MESH,
         )
 
     def pass_through(o):
         return pltpu.make_async_remote_copy(
             src_ref=yru.at[o - 1], dst_ref=yhu.at[o - 1],
-            send_sem=y_send.at[1 + o], recv_sem=y_sem.at[nt + o],
+            send_sem=u_send.at[0], recv_sem=l_sem.at[1],
             device_id=device(t=opposite(o)), device_id_type=MESH,
         )
 
@@ -206,11 +211,11 @@
 
     def hear_line(r):
         if r < line_rounds:
-            pl.semaphore_wait(line_sem.at[r], on_line)
+            pl.semaphore_wait(line_sem.at[r % 2], on_line)
 
     def next_line(r):
         if r < line_rounds:
-            tell_line(line_sem.at[r])
+            tell_line(line_sem.at[r % 2])
 
     w_epin.start()
     for o in range(1, nt):
@@ -224,7 +229,6 @@
     for o in range(1, nt):
         load_ea(o, 1, micro - 1, 1).start()
     w_pin.start()
-    w_ids.start()
     acc[...] = jnp.zeros_like(acc)
 
     def expert_out(o, m, e0, count):
@@ -237,6 +241,7 @@
     for o in range(1, nt):
         load_ea(o, 0, 1, 0).wait()
         expert_out(o, 0, 0, half)
+    w_ids.start()
     pl.semaphore_wait(barrier, nt - 1 + ne - 1 + stride - 1 + on_line)
     for o in range(1, nt):
         send_e(o, 0, 0, half).start()
@@ -274,7 +279,7 @@
         for first in range(0, micro, batch):
             for o in range(1, nt):
                 dsend[o - 1, pl.ds((l * micro + first) * q, batch * q)] = jnp.dot(
-                    va[o, l, first : first + batch].reshape(batch * q, pin.shape[1]), vpin[l],
+                    va[o * layers + l, first : first + batch].reshape(batch * q, pin.shape[1]), vpin[l],
                     preferred_element_type=jnp.float32,
                 )
 
@@ -282,16 +287,16 @@
             def _(i):
                 j = (l * micro + first) * PIECES + i
                 for o in range(1, nt):
-                    kept = (giver & (j >= LENT) & (j < ACROSS)) | (over & (j == ACROSS))
-
-                    @pl.when((j >= lent) & ~kept)
+
+                    @pl.when(~kept(j))
                     def _():
                         send_d(o, j).start()
 
-                    @pl.when(giver & (j == ACROSS - 1))
+                    @pl.when(giver & (j == FIRST - 1))
                     def _():
                         give_u(o).start()
 
+    w_ids.wait()
     load_ea(0, 0, micro, 0).start()
     load_ec.start()
 
@@ -311,8 +316,6 @@
     w_dval.wait()
     w_epout.start()
     w_eval.start()
-    w_ids.wait()
-    w_prior.start()
 
     lanes = rows.shape[2]
     lane = lax.broadcasted_iota(jnp.int32, (1, lanes), 1)
@@ -322,7 +325,8 @@
 
     for j in range(LENT):
         mask[j] = domain_of(j // PIECES % micro)
-    mask[LENT] = domain_of(ACROSS // PIECES % micro)
+    for j in range(FIRST, CROWD):
+        mask[j - GIVEN] = domain_of(j // PIECES % micro)
 
     @pl.when(lent > 0)
     def _():
@@ -347,8 +351,7 @@
         acc[some] += jnp.sum(value.reshape(batch, -1, 8, rank), axis=1)
 
     for l in range(layers):
-        load_a(0, l).wait()
-        load_c(l).wait()
+        landed(va.at[pl.ds(0, 1 + dim // act.shape[3])], a_sem.at[l])
         if l == layers - 1:
             pl.semaphore_wait(row_sem, stride - 1)
             tell_tensor(tensor_sem)
@@ -356,7 +359,7 @@
         for first in range(0, micro, batch):
             some = slice(first, first + batch)
             u = jnp.dot(
-                va[0, l, some].reshape(batch * q, pin.shape[1]), vpin[l], preferred_element_type=jnp.float32
+                va[l, some].reshape(batch * q, pin.shape[1]), vpin[l], preferred_element_type=jnp.float32
             )
             w = jnp.dot(vc[l, some].reshape(batch * q, dim), vpout[l], preferred_element_type=jnp.float32)
             g = lax.dot_general(
@@ -372,13 +375,13 @@
                     def _():
                         lend_g(j).start()
 
-            if ACROSS - 1 in done:
+            if FIRST - 1 in done:
 
                 @pl.when(giver)
                 def _():
                     give_g().start()
 
-            if ACROSS in done:
+            if CROWD - 1 in done:
 
                 @pl.when(over)
                 def _():
@@ -386,6 +389,7 @@
 
     w_epout.wait()
     w_eval.wait()
+    w_prior.start()
     load_ea(0, 0, micro, 0).wait()
     load_ec.wait()
     pl.semaphore_wait(tensor_sem, nt - 1)
@@ -412,7 +416,7 @@
             @pl.when(guest)
             def _():
                 for o in range(1, nt):
-                    landed(yru.at[o - 1], y_sem.at[1 + o])
+                    landed(yru.at[o - 1], y_sem.at[o - 1])
                     pass_through(o).start()
 
     landed(erecv, e_sem)
@@ -424,33 +428,28 @@
 
     w_prior.wait()
 
-    def cross(o, j):
-        return drecv[o - 1, rows_of(j)] * dg[rows_of(j)]
+    def cross(o, j, count=1):
+        return drecv[o - 1, rows_of(j, count)] * dg[rows_of(j, count)]
 
     def total_of(value):
         return jnp.sum(jnp.sum(value, axis=1, keepdims=True), axis=0, keepdims=True)
 
-    for c in range(LENT):
-
-        @pl.when(lent == c)
+    rows[me] = jnp.zeros((1, lanes), jnp.float32)
+
+    masks = count_of(taken > 0) + count_of(guest)
+    for c in (1, 2):
+
+        @pl.when(masks == c)
         def _():
-            for o in range(1, nt):
-                landed(drecv.at[o - 1, rows_of(c, LENT - c)], d_sem.at[o - 1, 0])
-                for j in range(c, LENT):
-                    fold(j // PIECES % micro, cross(o, j))
-
-    rows[me] = jnp.zeros((1, lanes), jnp.float32)
+            landed(lmask.at[pl.ds(0, c)], l_sem.at[2])
 
     @pl.when(taken > 0)
     def _():
-        landed(lmask, l_sem.at[1])
         for c in range(1, LENT + 1):
 
             @pl.when(taken == c)
             def _():
-                landed(lg.at[rows_of(0, c)], l_sem.at[0])
-                for o in range(1, nt):
-                    landed(lu.at[o - 1, rows_of(0, c)], l_sem.at[1 + o])
+                landed(drecv.at[0, rows_of(0, nt * c)], l_sem.at[0])
 
         for j in range(LENT):
 
@@ -460,34 +459,33 @@
                 for o in range(1, nt):
                     both = lu[o - 1, rows_of(j)] * lg[rows_of(j)]
                     value = value + jnp.sum(both.reshape(-1, 8, rank), axis=0)
-                rows[me] += lmask[j] * total_of(value)
-
-    @pl.when(~giver)
-    def _():
-        for o in range(1, nt):
-            landed(drecv.at[o - 1, given], d_sem.at[o - 1, 1])
-            for j in range(LENT, ACROSS):
+                rows[me] += lmask[0, j] * total_of(value)
+
+    together = units - ALONE - lent - GIVEN * count_of(giver) - OVER * count_of(over)
+    for c in range(units - ALONE - CROWD, units - ALONE + 1):
+
+        @pl.when(together == c)
+        def _():
+            for o in range(1, nt):
+                landed(drecv.at[o - 1, rows_of(0, c)], d_sem.at[o - 1, 0])
+
+    full = -(-CROWD // PIECES)
+    for j in [*range(full * PIECES), *range((blocks - 1) * PIECES, units - ALONE)]:
+
+        @pl.when(~kept(j))
+        def _():
+            for o in range(1, nt):
                 fold(j // PIECES % micro, cross(o, j))
 
-    @pl.when(~over)
-    def _():
-        for o in range(1, nt):
-            landed(drecv.at[o - 1, rows_of(ACROSS)], d_sem.at[o - 1, 2])
-            fold(ACROSS // PIECES % micro, cross(o, ACROSS))
-
-    for o in range(1, nt):
-        landed(drecv.at[o - 1, rows_of(CROWD, units - ALONE - CROWD)], d_sem.at[o - 1, 3])
-
-    @pl.loop(CROWD, units - ALONE)
-    def _(j):
-        for o in range(1, nt):
-            fold(lax.rem(lax.div(j, PIECES), micro), cross(o, j))
+    @pl.loop(full, blocks - 1)
+    def _(k):
+        for o in range(1, nt):
+            fold(lax.rem(k, micro), cross(o, k * PIECES, PIECES))
 
     def take(o, j):
-        landed(drecv.at[o - 1, rows_of(j)], d_sem.at[o - 1, j - units + ALONE + 4])
+        landed(drecv.at[o - 1, rows_of(j)], d_sem.at[o - 1, j - units + ALONE + 1])
 
     def take_given(o, i):
-        landed(hu.at[o - 1, rows_of(i)], hu_sem.at[o - 1, i])
         return hu[o - 1, rows_of(i)] * hg[rows_of(i)]
 
     def shorter(value):
@@ -501,32 +499,35 @@
 
     @pl.when(guest)
     def _():
-        landed(ymask, y_sem.at[1])
-        landed(yhg, y_sem.at[0])
-        value = jnp.zeros((8, rank), jnp.float32)
-        for o_ in range(1, nt):
-            landed(yhu.at[o_ - 1], y_sem.at[nt + o_])
-            value = value + shorter(yhu[o_ - 1] * yhg[...])
-        rows[me] += ymask[...] * total_of(value)
+        landed(drecv.at[0, rows_of(0, nt * OVER)], l_sem.at[1])
+        for i in range(OVER):
+            value = jnp.zeros((8, rank), jnp.float32)
+            for o_ in range(1, nt):
+                value = value + shorter(yhu[o_ - 1, rows_of(i)] * yhg[rows_of(i)])
+            rows[me] += lmask[1, LENT + i] * total_of(value)
 
     @pl.when(helper)
     def _():
         take(o, j)
         fold(micro - 1, cross(o, j))
         landed(hg, r_sem.at[0])
-        for i in range(GIVEN):
-            for o_ in range(1, nt):
-                if (i, o_) != (GIVEN - 1, nt - 1):
-                    fold((LENT + i) // PIECES % micro, take_given(o_, i))
+        for o_ in range(1, nt):
+            landed(hu.at[o_ - 1, rows_of(0, GIVEN - 1)], hu_sem.at[o_ - 1, 0])
+            for i in range(GIVEN - 1):
+                fold((LENT + i) // PIECES % micro, take_given(o_, i))
+        for o_ in range(1, nt - 1):
+            landed(hu.at[o_ - 1, rows_of(GIVEN - 1)], hu_sem.at[o_ - 1, 1])
+            fold((FIRST - 1) // PIECES % micro, take_given(o_, GIVEN - 1))
 
     part = rows[me]
     for m in range(micro):
         part = part + domain_of(m) * total_of(acc[m])
     rows[me] = part
-    chosen = jnp.where(helper, domain_of((ACROSS - 1) // PIECES % micro), domain_of(micro - 1))
+    chosen = jnp.where(helper, domain_of((FIRST - 1) // PIECES % micro), domain_of(micro - 1))
 
     @pl.when(helper)
     def _():
+        landed(hu.at[nt - 2, rows_of(GIVEN - 1)], hu_sem.at[nt - 2, 1])
         fin[...] = shorter(take_given(nt - 1, GIVEN - 1))
 
     @pl.when(~helper)
@@ -546,31 +547,20 @@
         landed(dsend.at[o - 1], s_sem.at[0])
     landed(esend, s_sem.at[1])
 
-    @pl.when(lent > 0)
-    def _():
-        lend_mask().wait_send()
-        for c in range(1, LENT + 1):
-
-            @pl.when(lent == c)
-            def _():
-                landed(dg.at[rows_of(0, c)], lg_send.at[0])
-
-    @pl.when(giver)
-    def _():
-        give_g().wait_send()
-
-    @pl.when(helper)
-    def _():
-        landed(ru, r_send)
-    @pl.when(over)
-    def _():
-        pass_over_mask().wait_send()
-        pass_over_g().wait_send()
-
-    @pl.when(guest)
-    def _():
-        for o in range(1, nt):
-            pass_through(o).wait_send()
+    masks = count_of(lent > 0) + count_of(over)
+    for c in (1, 2):
+
+        @pl.when(masks == c)
+        def _():
+            landed(lmask.at[pl.ds(0, c)], u_send.at[1])
+
+    sent = lent + GIVEN * (count_of(giver) + (nt - 1) * count_of(helper))
+    sent = sent + OVER * (count_of(over) + (nt - 1) * count_of(guest))
+    for c in range(1, LENT + (nt - 1) * (GIVEN + OVER) + 1):
+
+        @pl.when(sent == c)
+        def _():
+            landed(drecv.at[0, rows_of(0, c)], u_send.at[0])
 
     others = rows.at[pl.ds(0, n - 1)]
     landed(others, row_recv)
@@ -594,7 +584,7 @@
     experts, qc, hidden = ecot.shape[1], ecot.shape[2], eact.shape[3]
     domains = prior.shape[0]
     lanes = -(-domains // 128) * 128
-    lent, given = LENT * (q // PIECES), GIVEN * (q // PIECES)
+    lent, given, over = (units * (q // PIECES) for units in (LENT, GIVEN, OVER))
     bf, f32 = jnp.bfloat16, jnp.float32
     V, dma, regular = pltpu.VMEM, pltpu.SemaphoreType.DMA, pltpu.SemaphoreType.REGULAR
     logs = pl.pallas_call(
@@ -603,7 +593,7 @@
         in_specs=[pl.BlockSpec(memory_space=pltpu.HBM)] * 12,
         out_specs=pl.BlockSpec(memory_space=pltpu.VMEM),
         scratch_shapes=[
-            V((nt, layers, micro, q, feat), bf),
+            V((nt * layers, micro, q, feat), bf),
             V((layers, micro, q, dim), bf),
             V(pin.shape, bf),
             V(pout.shape, bf),
@@ -623,35 +613,31 @@
             V((micro, experts * qc, rank), f32),
             V((nt - 1, lent, rank), f32),
             V((lent, rank), f32),
-            V((LENT, 1, lanes), f32),
-            V((LENT + 1, 1, lanes), f32),
+            V((2, LENT + OVER, 1, lanes), f32),
+            V((LENT + OVER, 1, lanes), f32),
             V((nt - 1, given, rank), f32),
             V((nt - 1, given, rank), f32),
             V((given, rank), f32),
-            V((nt - 1, q // PIECES, rank), f32),
-            V((nt - 1, q // PIECES, rank), f32),
-            V((q // PIECES, rank), f32),
-            V((1, lanes), f32),
+            V((nt - 1, over, rank), f32),
+            V((nt - 1, over, rank), f32),
+            V((over, rank), f32),
             V((micro, 8, rank), f32),
             V((8, rank), f32),
             V((n, 1, lanes), f32),
             dma((layers,)),
-            dma((layers,)),
             dma((2,)),
+            dma((2,)),
+            dma((2,)),
+            dma,
+            dma((nt - 1, 1 + ALONE)),
             dma((3,)),
             dma((2,)),
-            dma,
-            dma((nt - 1, 4 + ALONE)),
-            dma((1 + nt,)),
-            dma((3,)),
             dma((nt,)),
-            dma((nt - 1, GIVEN)),
-            dma,
-            dma((2 * nt,)),
-            dma((1 + nt,)),
+            dma((nt - 1, 2)),
+            dma((nt - 1,)),
             dma,
             dma,
-            regular((max(places - 1, 1),)),
+            regular((2,)),
             regular,
             regular,
         ],

time: 27.4 us -> 26.7 us (0.974)
  Pallas kernels: 26.7 us -> 25.9 us
    pallas_call x1, Pallas kernels: 26.7 us -> 25.9 us  [per_device(): pl.pallas_call(functools.partial(kernel, sizes), out_shape=pltpu.VMEM((1,...]
where the time goes in v4:
time: 26.7 us; the launch traced here: 26.5 us
  Pallas kernels  25.9 us (97%)
  local copies, waits for them, and re-layouts  0.59 us (2%)
    pallas_call x1, Pallas kernels, per_device(): pl.pallas_call(functools.partial(kernel, sizes), out_shape=pltpu.VMEM((1,...  25.9 us
    dynamic_slice x1, local copies, waits for them, and re-layouts, per_device(): lax.dynamic_slice_in_dim(logs[0], lax.axis_index('dp') * share, share, 0)  0.59 us

profile of v4, /device:TPU:0, one launch (start us, length us, event | category | flops | bytes accessed | tf_op | source)
XLA Modules:
  0.0 26.5 jit_solution(5195761275080824189)
XLA Ops:
  0.0 25.9 %align.1 = f32[1,64]{1,0:T(1,128)S(1)} custom-call(bf16[2,4,256,1792]{3,2,1,0:T(8,128)(2,1)} %act.1, bf16[2,4,128,3584]{3,2,1,0:T(8,128)(2,1)} %cot.1, bf16[2,1792,128]{2,1,0:T(8,128)(2,1)} %pin.1, bf16[2,3584,128]{2,1,0:T(8,128)(2,1)} %pout.1, bf16[4,4,64,1280]{3,2,1,0:T(8,128)(2,1)} %eact.1, bf16[4,4,32,3584]{3,2,1,0:T(8,128)(2,1)} %ecot.1, ...), custom_call_target="tpu_custom_call" | custom-call | tf_op jit(solution)/shard_map/align/pallas_call | solution.py:590
  25.9 0.6 %dynamic-slice_bitcast_fusion = f32[8]{0:T(128)} fusion(f32[1,64]{1,0:T(1,128)S(1)} %align.1, s32[]{:T(128)S(6)} %select_n.3), kind=kLoop, calls=%fused_computation | loop fusion | bytes 68 | tf_op jit(solution)/shard_map/dynamic_slice | solution.py:650

commit v5 on v4

--- a/solution.py
+++ b/solution.py
@@ -12,7 +12,7 @@
 BATCH = 2
 PIECES = 4
 LENT = 5
-GIVEN = 6
+GIVEN = 7
 OVER = 2
 FIRST = LENT + GIVEN
 CROWD = FIRST + OVER
@@ -46,6 +46,7 @@
     h = q // PIECES
     blocks = layers * micro
     units = blocks * PIECES
+    full = -(-CROWD // PIECES)
     batch = BATCH if micro % BATCH == 0 else 1
     mate = (places - 1 - place) * stride + row
 
@@ -97,10 +98,10 @@
     def opposite(o):
         return lax.rem(tx + o, nt)
 
-    def send_d(o, j):
+    def send_d(o, j, count=1):
         i = jnp.maximum(j - (units - ALONE - 1), 0)
         return pltpu.make_async_remote_copy(
-            src_ref=dsend.at[o - 1, rows_of(j)], dst_ref=drecv.at[o - 1, rows_of(j)],
+            src_ref=dsend.at[o - 1, rows_of(j, count)], dst_ref=drecv.at[o - 1, rows_of(j, count)],
             send_sem=s_sem.at[0], recv_sem=d_sem.at[o - 1, i],
             device_id=device(t=opposite(o)), device_id_type=MESH,
         )
@@ -288,7 +289,13 @@
                 j = (l * micro + first) * PIECES + i
                 for o in range(1, nt):
 
-                    @pl.when(~kept(j))
+                    whole = (j >= full * PIECES) & (j < (blocks - 1) * PIECES)
+
+                    @pl.when(whole & (lax.rem(j, PIECES) == 0))
+                    def _():
+                        send_d(o, j, PIECES).start()
+
+                    @pl.when(~(whole | kept(j)))
                     def _():
                         send_d(o, j).start()
 
@@ -469,7 +476,6 @@
             for o in range(1, nt):
                 landed(drecv.at[o - 1, rows_of(0, c)], d_sem.at[o - 1, 0])
 
-    full = -(-CROWD // PIECES)
     for j in [*range(full * PIECES), *range((blocks - 1) * PIECES, units - ALONE)]:
 
         @pl.when(~kept(j))

time: 26.7 us -> 26.6 us (level)
  no operation moved by 1% of the time
where the time goes in v5:
time: 26.6 us; the launch traced here: 26.5 us
  Pallas kernels  25.9 us (97%)
  local copies, waits for them, and re-layouts  0.59 us (2%)
    pallas_call x1, Pallas kernels, per_device(): pl.pallas_call(functools.partial(kernel, sizes), out_shape=pltpu.VMEM((1,...  25.9 us
    dynamic_slice x1, local copies, waits for them, and re-layouts, per_device(): lax.dynamic_slice_in_dim(logs[0], lax.axis_index('dp') * share, share, 0)  0.59 us

profile of v5, /device:TPU:0, one launch (start us, length us, event | category | flops | bytes accessed | tf_op | source)
XLA Modules:
  0.0 26.5 jit_solution(14686524612295152471)
XLA Ops:
  0.0 25.9 %align.1 = f32[1,64]{1,0:T(1,128)S(1)} custom-call(bf16[2,4,256,1792]{3,2,1,0:T(8,128)(2,1)} %act.1, bf16[2,4,128,3584]{3,2,1,0:T(8,128)(2,1)} %cot.1, bf16[2,1792,128]{2,1,0:T(8,128)(2,1)} %pin.1, bf16[2,3584,128]{2,1,0:T(8,128)(2,1)} %pout.1, bf16[4,4,64,1280]{3,2,1,0:T(8,128)(2,1)} %eact.1, bf16[4,4,32,3584]{3,2,1,0:T(8,128)(2,1)} %ecot.1, ...), custom_call_target="tpu_custom_call" | custom-call | tf_op jit(solution)/shard_map/align/pallas_call | solution.py:596
  25.9 0.6 %dynamic-slice_bitcast_fusion = f32[8]{0:T(128)} fusion(f32[1,64]{1,0:T(1,128)S(1)} %align.1, s32[]{:T(128)S(6)} %select_n.3), kind=kLoop, calls=%fused_computation | loop fusion | bytes 68 | tf_op jit(solution)/shard_map/dynamic_slice | solution.py:656
